TPU v7x, 32 devices: a whole 2x2x4 slice. The times are simulated.
32 devices in a mesh: outer: 4 (over x, core), chip: 8 (over z, y).
Axes of the slice: x: 2, y: 2, z: 4, core: 2. Of those that a mesh axis runs over, the one named last changes fastest.
Arguments:
- inputs: bfloat16 [4096, 2048], P(('outer', 'chip')), may hold values from -6 to 6
- out_grads: bfloat16 [4096, 2048], P(('outer', 'chip')), may hold values from -6 to 6
- weight: bfloat16 [2048, 2048], P('chip'), may hold values from -0.125 to 0.125
- start_basis: float32 [64, 2048], P('chip'), may hold values from -6 to 6
- error_buffer: float32 [4, 2048, 2048], P('outer', 'chip'), may hold values from -2 to 2
Outputs:
- outputs: bfloat16 [4096, 2048], P(('outer', 'chip'))
- new_error: float32 [4, 2048, 2048], P('outer', 'chip')
All inputs are finite; a program needn't handle non-finite values.
Results may differ from a plain program's by a relative error of at most 0.0085.
Values may be sent and summed in bfloat16 or wider, within the bound.
A program may use at most 128 MiB of HBM per device.

v0:
```python
import jax
import jax.numpy as jnp
from jax import lax
from jax.sharding import PartitionSpec as P

TOK_DEV = 128


LEARNING_RATE = 0.2


def orthonormal(projected):
    finished = []
    for index in range(projected.shape[-2]):
        vector = projected[..., index, :]
        for unit in finished:
            vector = vector - jnp.sum(vector * unit, axis=-1, keepdims=True) * unit
        finished.append(vector / jnp.sqrt(jnp.sum(vector * vector, axis=-1, keepdims=True) + 1.0))
    return jnp.stack(finished, axis=-2)


def shards(inputs, out_grads, weight, start_basis, error_buffer):
    highest = lax.Precision.HIGHEST
    shard_rows = weight.shape[0]
    inner_dim = weight.shape[1]
    rank_count = start_basis.shape[0]
    pod_count = lax.axis_size("outer")
    columns = inputs
    gradient = (
        lax.psum_scatter(
            lax.dot_general(
                columns, out_grads, (((0,), (0,)), ((), ())), preferred_element_type=jnp.float32
            ),
            "chip",
            scatter_dimension=0,
            tiled=True,
        )
        / TOK_DEV
    )
    merged = gradient + error_buffer[0]
    projected = lax.dot_general(
        start_basis,
        merged,
        (((1,), (1,)), ((), ())),
        precision=highest,
        preferred_element_type=jnp.float32,
    )
    projected = lax.psum(projected, "outer") / pod_count
    left_basis = orthonormal(projected)
    right_factor = jnp.dot(
        left_basis, merged, precision=highest, preferred_element_type=jnp.float32
    )
    right_factor = (
        lax.psum(right_factor.astype(jnp.bfloat16), "outer").astype(jnp.float32) / pod_count
    )
    approx = lax.dot_general(
        left_basis,
        right_factor,
        (((0,), (0,)), ((), ())),
        precision=highest,
        preferred_element_type=jnp.float32,
    )
    new_error = (merged - approx)[None]
    all_basis, all_right = (
        lax.all_gather(left_basis, "chip", axis=1, tiled=True),
        lax.all_gather(right_factor, "chip", axis=0, tiled=True),
    )
    block_rows = lax.all_gather(weight, "chip", axis=0, tiled=True)
    length = block_rows.shape[0]
    owned = length // shard_rows
    left_rows = all_basis.reshape(rank_count, owned, shard_rows)
    right_rows = all_right.reshape(owned, rank_count, inner_dim)
    approx_rows = jnp.einsum("kns,nki->nsi", left_rows, right_rows, precision=highest).reshape(
        length, inner_dim
    )
    fresh_rows = (block_rows.astype(jnp.float32) - LEARNING_RATE * approx_rows).astype(jnp.bfloat16)
    columns = inputs
    result = jnp.dot(columns, fresh_rows, preferred_element_type=jnp.float32)
    return (result.astype(jnp.bfloat16), new_error)


def solution(mesh):
    return jax.shard_map(
        shards,
        mesh=mesh,
        in_specs=(
            P(("outer", "chip"), None),
            P(("outer", "chip"), None),
            P("chip", None),
            P("chip", None),
            P("outer", "chip", None),
        ),
        out_specs=(P(("outer", "chip"), None), P("outer", "chip", None)),
        check_vma=False,
    )
```

profile of v0, /device:TPU:0, one launch (start us, length us, event | category | flops | bytes accessed | tf_op | source)
XLA Modules:
  0.0 488.0 jit_solution(16077604721001273682)
XLA Ops:
  7.2 1.0 copy-done
  8.2 9.1 %fusion.6 = f32[2048,2048]{1,0:T(8,128)} fusion(bf16[128,2048]{1,0:T(8,128)(2,1)S(1)} %copy-done, bf16[128,2048]{1,0:T(8,128)(2,1)} %param.6), kind=kOutput, calls=%fused_computation.92 | convolution fusion | flops 1073741824 | bytes 17825792 | tf_op jit(solution)/shard_map/dot_general | solution.py:31
  17.4 0.0 all-gather.2.cloned.1.call-start
  17.4 0.7 all-gather.2.cloned.1.call-update
  18.1 281.6 %reduce-scatter.2.cloned.1.call-done = f32[256,2048]{1,0:T(8,128)} async-done(((f32[2048,2048]{1,0:T(8,128)}), f32[256,2048]{1,0:T(8,128)}) %reduce-scatter.2.cloned.1.call-update) | async-done | bytes 2097168 | tf_op jit(solution)/shard_map/reduce_scatter | solution.py:30
  299.8 3.3 convolution_bitcast_fusion
  303.1 6.4 %psum.14 = f32[8,256]{1,0:T(8,128)S(1)} all-reduce(f32[8,256]{1,0:T(8,128)S(1)} %convolution_bitcast_fusion), channel_id=1, replica_groups=mesh['outer'=4,'chip'=8] {'outer'}, use_global_device_ids=true, to_apply=%region_1.0 | all-reduce | flops 2048 | bytes 16384 | tf_op jit(solution)/shard_map/psum | solution.py:48
  309.5 0.6 multiply_reduce_fusion.35
  310.8 0.6 multiply_reduce_fusion.34
  311.4 1.3 multiply_reduce_fusion.7
  313.4 5.1 %multiply_reduce_fusion.6 = (f32[]{:T(128)}, f32[]{:T(128)}, f32[]{:T(128)}, f32[]{:T(128)}, f32[]{:T(128)}, /*index=5*/f32[]{:T(128)}, f32[256]{0:T(256)S(1)}) fusion(f32[256]{0:T(256)S(1)} %bitcast.44, f32[256]{0:T(256)S(1)} %bitcast.39, f32[]{:T(128)} %get-tuple-element.24, f32[256]{0:T(256)S(1)} %bitcast.47, f32[]{:T(128)} %get-tuple-element.25, ...), kind=kLoop, calls=%fused_computation.25 | loop fusion | flops 6906 | bytes 9272 | tf_op jit(solution)/shard_map/reduce_sum | solution.py:17
  318.5 1.9 multiply_reduce_fusion.30
  321.0 1.9 multiply_reduce_fusion.27
  323.0 6.3 %multiply_reduce_fusion.5 = (f32[]{:T(128)}, f32[]{:T(128)}, f32[]{:T(128)}, f32[]{:T(128)}, f32[]{:T(128)}, /*index=5*/f32[256]{0:T(256)S(1)}, f32[256]{0:T(256)S(1)}, f32[256]{0:T(256)S(1)}, f32[256]{0:T(256)S(1)}) fusion(f32[256]{0:T(256)S(1)} %get-tuple-element.57, f32[256]{0:T(256)S(1)} %get-tuple-element.56, f32[]{:T(128)} %get-tuple-element.55, ...), kind=kLoop, calls=%fused_computation.23 | loop fusion | flops 7163 | bytes 12344 | tf_op jit(solution)/shard_map/reduce_sum | solution.py:17
  329.9 3.8 multiply_reduce_fusion.4
  333.7 2.0 multiply_reduce_fusion.21
  336.4 1.8 multiply_reduce_fusion.16
  338.2 3.8 multiply_reduce_fusion.3
  342.7 2.5 multiply_reduce_fusion.2
  345.2 1.9 multiply_reduce_fusion.8
  347.8 1.8 multiply_reduce_fusion.1
  349.6 1.3 multiply_reduce_fusion
  351.6 17.5 %subtract_divide_fusion = (f32[1,256]{1,0:T(1,128)S(1)}, f32[1,256]{1,0:T(1,128)S(1)}, f32[1,256]{1,0:T(1,128)S(1)}, f32[1,256]{1,0:T(1,128)S(1)}, f32[1,256]{1,...) fusion(f32[1,256]{1,0:T(1,128)S(1)} %get-tuple-element.62, f32[]{:T(128)S(6)} %sqrt.39, f32[]{:T(128)} %get-tuple-element.38, ...), kind=kLoop, calls=%fused_computation.14 | loop fusion | flops 16128 | bytes 15500 | tf_op jit(solution)/shard_map/div | solution.py:18
  369.1 31.8 %all_gather.10 = f32[8,2048]{1,0:T(8,128)S(1)} all-gather(f32[8,256]{1,0:T(8,128)S(1)} %stack.2), channel_id=1, replica_groups=mesh['outer'=4,'chip'=8] {'chip'}, dimensions={1}, use_global_device_ids=true | all-gather | bytes 73728 | tf_op jit(solution)/shard_map/all_gather | solution.py:65
  400.9 3.0 convolution_convert_fusion.1
  403.9 11.1 %psum.15 = bf16[8,2048]{1,0:T(8,128)(2,1)S(1)} all-reduce(bf16[8,2048]{1,0:T(8,128)(2,1)S(1)} %convolution_convert_fusion.1), channel_id=1, replica_groups=mesh['outer'=4,'chip'=8] {'outer'}, use_global_device_ids=true, to_apply=%region_38.0 | all-reduce | flops 16384 | bytes 65536 | tf_op jit(solution)/shard_map/psum | solution.py:54
  415.0 32.4 %all_gather.11 = f32[64,2048]{1,0:T(8,128)S(1)} all-gather(f32[8,2048]{1,0:T(8,128)S(1)} %convert_multiply_fusion), channel_id=1, replica_groups=mesh['outer'=4,'chip'=8] {'chip'}, dimensions={0}, use_global_device_ids=true | all-gather | bytes 589824 | tf_op jit(solution)/shard_map/all_gather | solution.py:66
  447.4 16.2 %broadcast_multiply_fusion = f32[8,256,2048]{2,1,0:T(8,128)} fusion(f32[8,8,256]{2,0,1:T(8,128)S(1)} %bitcast.36, f32[64,2048]{1,0:T(8,128)S(1)} %all_gather.11), kind=kOutput, calls=%fused_computation.2 | convolution fusion | flops 406847488 | bytes 17367040 | tf_op jit(solution)/shard_map/kns,nki->nsi/dot_general | solution.py:73
  463.6 9.2 %fusion = bf16[2048,2048]{1,0:T(8,128)(2,1)S(1)} fusion(f32[8,256,2048]{2,1,0:T(8,128)} %broadcast_multiply_fusion, bf16[2048,2048]{1,0:T(8,128)(2,1)} %all-gather.2.cloned.1.call-done), kind=kLoop, calls=%fused_computation.1 | loop fusion | flops 12582912 | bytes 33554432 | tf_op jit(solution)/shard_map/convert_element_type | solution.py:76
  472.8 2.5 fusion.2
  475.3 1.0 copy.7
  476.3 4.9 fusion.1
  (12 shorter events, 0.1 us)
Async XLA Ops:
  7.2 1.0 copy-start
  7.2 292.6 %reduce-scatter.2.cloned.1.call-start = ((), (), s32[]{:S(2)}) async-start(), calls=%async_computation.2 | async-start | bytes 18874368 | tf_op jit(solution)/shard_map/reduce_scatter | solution.py:30
  17.3 282.4 %copy-start.1 = (f32[1,256,2048]{2,1,0:T(8,128)S(1)}, f32[1,256,2048]{2,1,0:T(8,128)}, u32[]{:S(2)}) copy-start(f32[1,256,2048]{2,1,0:T(8,128)} %param.9) | copy-start | bytes 6291460
  17.3 282.4 %copy-start.2 = (f32[8,2048]{1,0:T(8,128)S(1)}, f32[8,2048]{1,0:T(8,128)}, u32[]{:S(2)}) copy-start(f32[8,2048]{1,0:T(8,128)} %param.8) | copy-start | bytes 196612
  17.4 446.3 %all-gather.2.cloned.1.call-start = ((), (), s32[]{:S(2)}) async-start(), calls=%async_computation.1 | async-start | bytes 9437184 | tf_op jit(solution)/shard_map/all_gather | solution.py:68
Sparse Core Ops, SparseCore 0:
  17.5 282.2 reduce-scatter.1
  301.9 127.1 all-gather.1
where the time goes:
time: 489 us; the launch traced here: 488 us
  waiting for transfers between devices  282 us (58%)
  blocking collectives  81.6 us (17%)
  other arithmetic  63.3 us (13%)
  matrix products  39 us (8%)
  between operations  19.7 us (4%)
    reduce_scatter x1, waiting for transfers between devices, shards(): lax.psum_scatter(lax.dot_general(columns, out_grads, (((0,), (0,)), ((),...  282 us
    all_gather x1, blocking collectives, shards(): lax.all_gather(right_factor, 'chip', axis=0, tiled=True)  32.4 us
    all_gather x1, blocking collectives, shards(): lax.all_gather(left_basis, 'chip', axis=1, tiled=True)  31.8 us
    reduce_sum x10, other arithmetic, orthonormal(): vector = vector - jnp.sum(vector * unit, axis=-1, keepdims=True) * unit  29 us
    div x1, other arithmetic, orthonormal(): vector / jnp.sqrt(jnp.sum(vector * vector, axis=-1, keepdims=True) + 1.0)  17.5 us
    dot_general x1, matrix products, shards(): jnp.einsum('kns,nki->nsi', left_rows, right_rows, precision=highest)  16.2 us
    psum x1, blocking collectives, shards(): lax.psum(right_factor.astype(jnp.bfloat16), 'outer').astype(jnp.float32)  11.1 us
  transfers between devices with their start and end apart: 2, of which 1 were waited for; matrix products, arithmetic and copies ran while one was open for 16% of the time, Pallas kernels for 0%

commit v1 on v0

v1 whole, which is shorter than its diff:
```python
import functools

import jax
import jax.numpy as jnp
from jax import lax
from jax.experimental import pallas as pl
from jax.experimental.pallas import tpu as pltpu
from jax.sharding import PartitionSpec as P

TOK_DEV = 128
LEARNING_RATE = 0.2
CHUNKS = 4
F32 = jnp.float32
BF16 = jnp.bfloat16
HIGHEST = lax.Precision.HIGHEST


def dot(a, b, ca, cb, precision=None):
    return lax.dot_general(
        a, b, (((ca,), (cb,)), ((), ())), precision=precision, preferred_element_type=F32
    )


def orthonormal(v):
    count = v.shape[0]
    row = lax.broadcasted_iota(jnp.int32, (count, 1), 0)
    for k in range(count):
        pivot = v[k : k + 1, :]
        d = jnp.sum(v * pivot, axis=1, keepdims=True)
        norm = d[k : k + 1, :] + 1.0
        scale = jnp.where(row > k, d / norm, 0.0)
        unit = pivot / jnp.sqrt(norm)
        v = jnp.where(row == k, unit, v - scale * pivot)
    return v


def kernel(
    A, B, PODS,
    x_ref, g_ref, w_ref, basis_ref, err_ref,
    out_ref, ne_ref,
    xg, xt, gg, wq, ysend, yrecv, up_s, up_r, dn_s, dn_r,
    left_s, left_r, right_s, right_r, fl, fr,
    xs_sem, xr_sem, ws_sem, wr_sem, gs_sem, gr_sem, ys_sem, yr_sem, rs_sem, rr_sem,
    ls_sem, lr_sem, hs_sem, hr_sem, fs_sem, fq_sem,
):
    o = lax.axis_index("outer")
    c = lax.axis_index("chip")
    a, b = c // B, c % B
    NC = A * B
    T, N = g_ref.shape
    S = w_ref.shape[0]
    Q = B * S
    R = basis_ref.shape[0]
    K = CHUNKS
    CN = N // K
    cols = [pl.ds(k * CN, CN) for k in range(K)]

    def remote(src, dst, ss, rs, axis, index):
        return pltpu.make_async_remote_copy(
            src_ref=src, dst_ref=dst, send_sem=ss, recv_sem=rs,
            device_id={axis: index}, device_id_type=pl.DeviceIdType.MESH,
        )

    barrier = pltpu.get_barrier_semaphore()
    for d in range(1, NC):
        pl.semaphore_signal(
            barrier, inc=1, device_id={"chip": (c + d) % NC}, device_id_type=pl.DeviceIdType.MESH
        )
    for d in range(1, PODS):
        pl.semaphore_signal(
            barrier, inc=1, device_id={"outer": (o + d) % PODS}, device_id_type=pl.DeviceIdType.MESH
        )
    pl.semaphore_wait(barrier, NC - 1 + PODS - 1)

    def rows_of(s):
        return pl.ds(pl.multiple_of(s * T, T), T)

    def shard_of(s):
        return pl.ds(pl.multiple_of(s * S, S), S)

    x_copies = []
    for d in range(1, A):
        t = (a + d) % A
        x_copies.append(remote(
            x_ref.at[:, pl.ds(pl.multiple_of(t * Q, Q), Q)], xg.at[rows_of(a)],
            xs_sem.at[d], xr_sem.at[d], "chip", t * B + b,
        ))
    for cp in x_copies:
        cp.start()

    def g_copy(direction, h, k):
        step = 1 if direction == 0 else -1
        source = a - step * (h - 1)
        src = g_ref.at[:, cols[k]] if h == 1 else gg.at[rows_of(source), cols[k]]
        return remote(
            src, gg.at[rows_of(source), cols[k]],
            gs_sem.at[direction, h, k], gr_sem.at[direction, h, k], "chip", c + step * B,
        )

    def g_sends(direction, h):
        return (
            jnp.logical_and(a - (h - 1) >= 0, a + 1 < A)
            if direction == 0
            else jnp.logical_and(a + (h - 1) < A, a >= 1)
        )

    def g_gets(direction, h):
        return a - h >= 0 if direction == 0 else a + h < A

    def g_arrival(direction, h, k):
        step = 1 if direction == 0 else -1
        place = gg.at[rows_of(a - step * h), cols[k]]
        return remote(
            place, place, gs_sem.at[direction, h, k], gr_sem.at[direction, h, k], "chip",
            c - step * B,
        )

    for k in range(K):
        for direction in range(2):
            @pl.when(g_sends(direction, 1))
            def _():
                g_copy(direction, 1, k).start()

    w_copies = []
    for d in range(1, B):
        t = (b + d) % B
        w_copies.append(remote(
            w_ref, wq.at[shard_of(b)], ws_sem.at[d], wr_sem.at[d], "chip", a * B + t
        ))
    for cp in w_copies:
        cp.start()

    xg[rows_of(a), :] = x_ref[:, pl.ds(pl.multiple_of(a * Q, Q), Q)]
    gg[rows_of(a), :] = g_ref[...]
    wq[shard_of(b), :] = w_ref[...]
    for cp in x_copies:
        cp.wait_recv()
    xt[...] = xg[...].T

    def y_copy(d, k):
        t = (b + d) % B
        return remote(
            ysend.at[d, :, cols[k]], yrecv.at[d, :, cols[k]],
            ys_sem.at[d, k], yr_sem.at[d, k], "chip", a * B + t,
        )

    def gradient_chunk(k):
        for d in range(1, B):
            t = (b + d) % B
            part = dot(xt[shard_of(t), :], gg[:, cols[k]], 1, 0)
            ysend[d, :, cols[k]] = part.astype(BF16)
            y_copy(d, k).start()
        part = dot(xt[shard_of(b), :], gg[:, cols[k]], 1, 0)
        ne_ref[:, cols[k]] = part

    for wave in range(1, A - 1 + K):
        for h in range(1, A):
            k = wave - h
            if 0 <= k < K:
                for direction in range(2):
                    @pl.when(g_gets(direction, h))
                    def _():
                        g_arrival(direction, h, k).wait_recv()
                    if h + 1 < A:
                        @pl.when(g_sends(direction, h + 1))
                        def _():
                            g_copy(direction, h + 1, k).start()
        if 0 <= wave - (A - 1) < K:
            gradient_chunk(wave - (A - 1))

    def o_copy(direction, r, k):
        s_buf, r_buf = (up_s, up_r) if direction == 0 else (dn_s, dn_r)
        return remote(
            s_buf.at[r, :, cols[k]], r_buf.at[r, :, cols[k]],
            rs_sem.at[direction, r, k], rr_sem.at[direction, r, k], "chip",
            c + B if direction == 0 else c - B,
        )

    def o_sends(direction, r):
        return a + r < A if direction == 0 else a - r >= 0

    def o_gets(direction, r):
        if direction == 0:
            return jnp.logical_and(a >= 1, a - 1 + r < A)
        return jnp.logical_and(a + 1 < A, a + 1 - r >= 0)

    def out_stage(r):
        for k in range(K):
            for direction in range(2):
                s_buf, r_buf = (up_s, up_r) if direction == 0 else (dn_s, dn_r)

                @pl.when(o_sends(direction, r))
                def _():
                    token = a + r if direction == 0 else a - r
                    s_buf[r, :, cols[k]] = dot(xg[rows_of(token), :], wq[:, cols[k]], 1, 0).astype(BF16)
                    if r + 1 < A:
                        @pl.when(o_gets(direction, r + 1))
                        def _():
                            o_copy(direction, r + 1, k).wait_recv()
                            s_buf[r, :, cols[k]] = (
                                s_buf[r, :, cols[k]].astype(F32) + r_buf[r + 1, :, cols[k]].astype(F32)
                            ).astype(BF16)
                    o_copy(direction, r, k).start()

    for cp in w_copies:
        cp.wait_recv()
    out_stage(A - 1)

    total = None
    for k in range(K):
        part = ne_ref[:, cols[k]]
        for d in range(1, B):
            y_copy(d, k).wait_recv()
            part = part + yrecv[d, :, cols[k]].astype(F32)
        part = part / TOK_DEV + err_ref[:, cols[k]]
        ne_ref[:, cols[k]] = part
        piece = dot(basis_ref[:, cols[k]], part, 1, 1, HIGHEST)
        total = piece if total is None else total + piece
    left_s[...] = total
    l_copies = [
        remote(left_s, left_r.at[d], ls_sem.at[d], lr_sem.at[d], "outer", (o + d) % PODS)
        for d in range(1, PODS)
    ]
    for cp in l_copies:
        cp.start()
    for r in range(A - 2, 1, -1):
        out_stage(r)
    for d, cp in enumerate(l_copies):
        cp.wait_recv()
        total = total + left_r[d + 1]
    left = orthonormal(total / PODS)

    f_peers = [(c + d) % NC for d in range(1, NC)]
    fl[0] = left
    fl_copies = [
        remote(fl.at[0], fl.at[d + 1], fs_sem.at[0, d], fq_sem.at[0, d], "chip", t)
        for d, t in enumerate(f_peers)
    ]
    right = dot(left, ne_ref[...], 1, 0, HIGHEST).astype(BF16)
    right_s[...] = right
    h_copies = [
        remote(right_s, right_r.at[d], hs_sem.at[d], hr_sem.at[d], "outer", (o + d) % PODS)
        for d in range(1, PODS)
    ]
    for cp in h_copies:
        cp.start()
    for cp in fl_copies:
        cp.start()
    if A > 1:
        out_stage(1)
    right = right.astype(F32)
    for d, cp in enumerate(h_copies):
        cp.wait_recv()
        right = right + right_r[d + 1].astype(F32)
    right = right / PODS
    fr[0] = right.astype(BF16)
    fr_copies = [
        remote(fr.at[0], fr.at[d + 1], fs_sem.at[1, d], fq_sem.at[1, d], "chip", t)
        for d, t in enumerate(f_peers)
    ]
    for cp in fr_copies:
        cp.start()
    for k in range(K):
        ne_ref[:, cols[k]] = ne_ref[:, cols[k]] - dot(
            left, right[:, k * CN : (k + 1) * CN], 0, 0, HIGHEST
        )

    z_rows = []
    for d in range(NC):
        if d > 0:
            fl_copies[d - 1].wait_recv()
        owner = (c - d + NC) % NC
        z_rows.append(dot(fl[d], x_ref[:, shard_of(owner)].astype(F32), 1, 1, HIGHEST))
    z = jnp.concatenate(z_rows, axis=0)
    for cp in fr_copies:
        cp.wait_recv()
    for k in range(K):
        rights = jnp.concatenate([fr[d, :, cols[k]].astype(F32) for d in range(NC)], axis=0)
        delta = dot(z, rights, 0, 0, HIGHEST)
        for direction in range(2):
            r_buf = up_r if direction == 0 else dn_r

            @pl.when(o_gets(direction, 1))
            def _():
                o_copy(direction, 1, k).wait_recv()

            @pl.when(jnp.logical_not(o_gets(direction, 1)))
            def _():
                r_buf[1, :, cols[k]] = jnp.zeros((T, CN), BF16)
        mine = dot(xg[rows_of(a), :], wq[:, cols[k]], 1, 0)
        mine = mine + up_r[1, :, cols[k]].astype(F32) + dn_r[1, :, cols[k]].astype(F32)
        out_ref[:, cols[k]] = (mine - LEARNING_RATE * delta).astype(BF16)

    for cp in x_copies + w_copies + l_copies + h_copies + fl_copies + fr_copies:
        cp.wait_send()
    for k in range(K):
        for d in range(1, B):
            y_copy(d, k).wait_send()
        for direction in range(2):
            for h in range(1, A):
                @pl.when(g_sends(direction, h))
                def _():
                    g_copy(direction, h, k).wait_send()

                @pl.when(o_sends(direction, h))
                def _():
                    o_copy(direction, h, k).wait_send()


def shards(inputs, out_grads, weight, start_basis, error_buffer):
    PODS, NC = lax.axis_size("outer"), lax.axis_size("chip")
    A = 4 if NC % 4 == 0 else NC
    B = NC // A
    T, D = inputs.shape
    N = out_grads.shape[1]
    S = weight.shape[0]
    R = start_basis.shape[0]
    Q = B * S
    K = CHUNKS
    dma = pltpu.SemaphoreType.DMA
    vmem = pl.BlockSpec(memory_space=pltpu.VMEM)
    outputs, new_error = pl.pallas_call(
        functools.partial(kernel, A, B, PODS),
        out_shape=(
            jax.ShapeDtypeStruct((T, N), BF16),
            jax.ShapeDtypeStruct((S, N), F32),
        ),
        in_specs=[vmem] * 5,
        out_specs=(vmem, vmem),
        scratch_shapes=[
            pltpu.VMEM((A * T, Q), BF16),
            pltpu.VMEM((Q, A * T), BF16),
            pltpu.VMEM((A * T, N), BF16),
            pltpu.VMEM((Q, N), BF16),
            pltpu.VMEM((B, S, N), BF16),
            pltpu.VMEM((B, S, N), BF16),
            pltpu.VMEM((A, T, N), BF16),
            pltpu.VMEM((A, T, N), BF16),
            pltpu.VMEM((A, T, N), BF16),
            pltpu.VMEM((A, T, N), BF16),
            pltpu.VMEM((R, S), F32),
            pltpu.VMEM((PODS, R, S), F32),
            pltpu.VMEM((R, N), BF16),
            pltpu.VMEM((PODS, R, N), BF16),
            pltpu.VMEM((NC, R, S), F32),
            pltpu.VMEM((NC, R, N), BF16),
            dma((A,)), dma((A,)), dma((B,)), dma((B,)),
            dma((2, A, K)), dma((2, A, K)), dma((B, K)), dma((B, K)),
            dma((2, A, K)), dma((2, A, K)),
            dma((PODS,)), dma((PODS,)), dma((PODS,)), dma((PODS,)),
            dma((2, NC)), dma((2, NC)),
        ],
        compiler_params=pltpu.CompilerParams(
            collective_id=0, has_side_effects=True, vmem_limit_bytes=56 * 1024 * 1024
        ),
        name="step",
    )(inputs, out_grads, weight, start_basis, error_buffer[0])
    return outputs, new_error[None]


def solution(mesh):
    return jax.shard_map(
        shards,
        mesh=mesh,
        in_specs=(
            P(("outer", "chip"), None),
            P(("outer", "chip"), None),
            P("chip", None),
            P("chip", None),
            P("outer", "chip", None),
        ),
        out_specs=(P(("outer", "chip"), None), P("outer", "chip", None)),
        check_vma=False,
    )
```

time: 489 us -> 103 us (0.21)
  waiting for transfers between devices: 282 us -> 0 us
  Pallas kernels: 0 us -> 96 us
  blocking collectives: 81.6 us -> 0 us
  other arithmetic: 63.3 us -> 0 us
  matrix products: 39 us -> 0 us
  between operations: 19.7 us -> 0.64 us
    reduce_scatter x1 -> x0, waiting for transfers between devices: 282 us -> none  [shards(): lax.psum_scatter(lax.dot_general(columns, out_grads, (((0,), (0,)), ((),...]
    pallas_call x0 -> x1, Pallas kernels: none -> 96 us  [shards(): pl.pallas_call(functools.partial(kernel, A, B, PODS), out_shape=(jax.Shap...]
    all_gather x2 -> x0, blocking collectives: 64.2 us -> none  [the longest x1 32.4 us: shards(): lax.all_gather(right_factor, 'chip', axis=0, tiled=True)]
    dot_general x6 -> x0, matrix products: 39 us -> none  [the longest x1 16.2 us: shards(): jnp.einsum('kns,nki->nsi', left_rows, right_rows, precision=highest)]
    reduce_sum x15 -> x0, other arithmetic: 36.6 us -> none  [the longest x10 29 us: orthonormal(): vector = vector - jnp.sum(vector * unit, axis=-1, keepdims=True) * unit]
    div x3 -> x0, other arithmetic: 17.5 us -> none  [the longest x1 17.5 us: orthonormal(): vector / jnp.sqrt(jnp.sum(vector * vector, axis=-1, keepdims=True) + 1.0)]
    psum x2 -> x0, blocking collectives: 17.4 us -> none  [the longest x1 11.1 us: shards(): lax.psum(right_factor.astype(jnp.bfloat16), 'outer').astype(jnp.float32)]
    convert_element_type x1 -> x0, other arithmetic: 9.18 us -> none  [shards(): (block_rows.astype(jnp.float32) - LEARNING_RATE * approx_rows).astype(jnp...]
  transfers between devices with their start and end apart: 2 -> 0, of which waited for: 1 -> 0; matrix products, arithmetic and copies ran while one was open for 16% -> 0% of each run, Pallas kernels for 0% -> 0%
where the time goes in v1:
time: 103 us; the launch traced here: 102 us
  Pallas kernels  96 us (93%)
  local copies, waits for them, and re-layouts  5.02 us (5%)
    pallas_call x1, Pallas kernels, shards(): pl.pallas_call(functools.partial(kernel, A, B, PODS), out_shape=(jax.Shap...  96 us
    unnamed x2, local copies, waits for them, and re-layouts  5.02 us

profile of v1, /device:TPU:0, one launch (start us, length us, event | category | flops | bytes accessed | tf_op | source)
XLA Modules:
  0.0 101.6 jit_solution(17555658102139992342)
XLA Ops:
  0.6 96.0 %step.1 = (bf16[128,2048]{1,0:T(8,128)(2,1)}, f32[256,2048]{1,0:T(8,128)}) custom-call(bf16[128,2048]{1,0:T(8,128)(2,1)} %x_ref.1, bf16[128,2048]{1,0:T(8,128)(2,1)} %g_ref.1, bf16[256,2048]{1,0:T(8,128)(2,1)} %w_ref.1, f32[8,2048]{1,0:T(8,128)} %basis_ref.1, f32[256,2048]{1,0:T(8,128)} %bitcast.2), custom_call_target="tpu_custom_call" | custom-call | tf_op jit(solution)/shard_map/step/pallas_call | solution.py:322
  96.6 1.9 %copy.9 = bf16[128,2048]{1,0:T(8,128)(2,1)} copy(bf16[128,2048]{1,0:T(8,128)(2,1)} %get-tuple-element.8) | data formatting | bytes 1048576
  98.5 3.1 %copy.10 = f32[1,256,2048]{2,1,0:T(8,128)} copy(f32[1,256,2048]{2,1,0:T(8,128)} %bitcast.3) | data formatting | bytes 4194304
